TPU v7x, 256 devices: a whole 4x4x8 slice. The times are simulated.
256 devices in a mesh: samp: 64 (over y, z, core), gene: 4 (over x).
Axes of the slice: x: 4, y: 4, z: 8, core: 2. Of those that a mesh axis runs over, the one named last changes fastest.
Arguments:
- genotypes: int32 [2048, 32768], P('samp', 'gene'), may hold values from -2147483648 to 1789569706, as said below
- allele_freq: float32 [32768], P('gene'), may hold values from 0.035 to 0.56
- sample_weight: float32 [16, 2048], P(None, 'samp'), may hold values from 0.2 to 2
- residual: float32 [16, 2048], P(None, 'samp'), may hold values from -12 to 12
- variant_weight: float32 [32768], P('gene'), may hold values from 0.2 to 4
- block_gene: int32 [256], replicated, may hold values from 0 to 127, as said below
- gene_variants: int32 [128], replicated, may hold values from 1 to 384, as said below
Outputs:
- burden_z: float32 [128], replicated
- skat_z: float32 [128], replicated
Inputs may be any that keep to these rules, and one draw needn't show every extreme that they name: Each word holds 16 dosages 0, 1 or 2: bits 2k and 2k+1 of genotypes[i, v] are the dosage of variant slot v in sample (k, i); a dosage 2 in the top field sets the sign bit. `block_gene`: never falling; the blocks come in aligned groups of four, each shared by two consecutive genes, so every gene has 1 to 3 blocks. `gene_variants`: A gene with m blocks has from (m - 1) * 128 + 1 to m * 128 live variants; the slots after them in its last block are padding.
All inputs are finite; a program needn't handle non-finite values.
Results may differ from a plain program's by a relative error of at most 0.0037.
Values sent between devices are 32-bit elements; how exact they have to be, the bound alone decides.
A program may use at most 64 MiB of HBM per device.

v0:
```python
import jax
import jax.numpy as jnp
from jax import lax
from jax.sharding import Mesh
from jax.sharding import PartitionSpec as P

BLK = 128
SAMP = ("samp_0", "samp_1", "samp_2")
SAMP_GENE = ("samp_0", "samp_1", "samp_2", "gene")


def turned_gather(arrays, axis, dims):
    turned = [jnp.moveaxis(a, dim, 0) for a, dim in zip(arrays, dims)]
    both = jnp.concatenate([t.reshape(len(t), -1) for t in turned], axis=1)
    result, at, done = (lax.all_gather(both, axis, axis=0, tiled=True), 0, [])
    for t, dim in zip(turned, dims):
        share = result[:, at : at + t[0].size].reshape(-1, *t.shape[1:])
        done.append(jnp.moveaxis(share, 0, dim))
        at += t[0].size
    return tuple(done)


def by_axis(array, axes):
    for axis in axes:
        array = lax.psum(array, axis)
    return array


def unpack(packed_words, allele_part, root_weight):
    fields = root_weight.shape[0]
    offsets = 2 * jnp.arange(fields, dtype=jnp.int32)
    dosage = jnp.bitwise_and(jnp.right_shift(packed_words[None, :, :], offsets[:, None, None]), 3)
    centered = dosage.astype(jnp.float32) - 2.0 * allele_part[None, None, :]
    return (root_weight[:, :, None] * centered).astype(jnp.bfloat16)


def block_grams(scaled, block_count):
    stacked = scaled.reshape(scaled.shape[0] * scaled.shape[1], block_count, BLK)
    return jnp.einsum("sbu,sbv->buv", stacked, stacked, preferred_element_type=jnp.float32)


def block_stats(gram_part, scores, effective):
    weighted_score = effective * scores
    burden_sum = jnp.sum(weighted_score, axis=1)
    skat_sum = jnp.sum(weighted_score * weighted_score, axis=1)
    image = jnp.einsum("buv,bv->bu", gram_part, effective)
    burden_var = jnp.sum(effective * image, axis=1)
    diagonal = jnp.diagonal(gram_part, axis1=1, axis2=2)
    trace_one = jnp.sum(effective * effective * diagonal, axis=1)
    scaled_gram = effective[:, :, None] * gram_part * effective[:, None, :]
    trace_two = jnp.sum(scaled_gram * scaled_gram, axis=(1, 2))
    return jnp.stack([burden_sum, burden_var, skat_sum, trace_one, trace_two])


def live_weights(block_ids, variant_part, block_gene, gene_variants):
    total_blocks = block_gene.shape[0]
    genes = gene_variants.shape[0]
    chosen = block_ids[:, None] == jnp.arange(total_blocks, dtype=jnp.int32)[None, :]
    gene_of = jnp.sum(jnp.where(chosen, block_gene[None, :], 0), axis=1)
    first_block = jnp.sum((block_gene[None, :] < gene_of[:, None]).astype(jnp.int32), axis=1)
    member = gene_of[:, None] == jnp.arange(genes, dtype=jnp.int32)[None, :]
    counted = jnp.sum(jnp.where(member, gene_variants[None, :], 0), axis=1)
    column = jnp.arange(BLK, dtype=jnp.int32)
    is_live = (block_ids - first_block)[:, None] * BLK + column[None, :] < counted[:, None]
    return (variant_part * is_live.astype(jnp.float32), member.astype(jnp.float32))


def local(
    genotypes, allele_freq, sample_weight, residual, variant_weight, block_gene, gene_variants
):
    local_blocks = genotypes.shape[1] // BLK
    owned_count = local_blocks // lax.axis_size(SAMP)
    samp_index = lax.axis_index(SAMP)
    gene_index = lax.axis_index("gene")
    block_ids = (
        gene_index * local_blocks
        + samp_index * owned_count
        + jnp.arange(owned_count, dtype=jnp.int32)
    )
    variant_blocks = variant_weight.reshape(local_blocks, BLK)
    own_weights = lax.dynamic_slice_in_dim(variant_blocks, samp_index * owned_count, owned_count, 0)
    effective, member = live_weights(block_ids, own_weights, block_gene, gene_variants)
    own_words = lax.all_to_all(genotypes, SAMP, split_axis=1, concat_axis=0, tiled=True)
    all_weight, all_residual = turned_gather((sample_weight, residual), SAMP, (1, 1))
    own_freq = lax.dynamic_slice_in_dim(
        allele_freq, samp_index * owned_count * BLK, owned_count * BLK, 0
    )
    root_all = jnp.sqrt(all_weight)
    weighted_residual = (root_all * all_residual).astype(jnp.bfloat16)
    scaled = unpack(own_words, own_freq, root_all)
    gram_part = block_grams(scaled, owned_count)
    flattened = scaled.reshape(scaled.shape[0] * scaled.shape[1], owned_count * BLK)
    scores = jnp.dot(
        weighted_residual.reshape(1, -1), flattened, preferred_element_type=jnp.float32
    )
    variance = jnp.sum(all_weight * all_residual * all_residual) / (
        all_weight.shape[0] * all_weight.shape[1]
    )
    gene_parts = jnp.dot(block_stats(gram_part, scores, effective), member)
    totals = by_axis(gene_parts, SAMP_GENE)
    burden = totals[0] / jnp.sqrt(variance * totals[1])
    skat_score = (totals[2] - variance * totals[3]) / (variance * jnp.sqrt(2.0 * totals[4]))
    return (burden, skat_score)


def solution(mesh):
    torus = Mesh(
        mesh.devices.reshape(4, 8, 2, mesh.shape["gene"]), ("samp_0", "samp_1", "samp_2", "gene")
    )
    placed = (P(SAMP, "gene"), P("gene"), P(None, SAMP), P(None, SAMP), P("gene"), P(), P())
    return jax.shard_map(local, mesh=torus, in_specs=placed, out_specs=(P(), P()), check_vma=False)
```

profile of v0, /device:TPU:1, one launch (start us, length us, event | category | flops | bytes accessed | tf_op | source)
XLA Modules:
  0.0 155.8 jit_solution(2203239968844073498)
XLA Ops:
  0.6 0.0 copy-start
  0.6 0.0 copy-start.1
  0.7 1.2 copy-done
  1.9 1.1 copy_bitcast_fusion
  3.0 13.1 %all-to-all-start = ((s32[32,64,128]{2,0,1:T(8,128)}), s32[32,64,128]{2,0,1:T(8,128)S(1)}, u32[]{:S(2)}, u32[]{:S(2)}) async-start(s32[32,64,128]{2,0,1:T(8,128)} %copy_bitcast_fusion), calls=%async_computation | async-start | bytes 2097152 | tf_op jit(solution)/shard_map/all_to_all | solution.py:83
  16.2 1.3 fusion.19
  17.5 2.0 %fusion.20 = s32[]{:T(128)} fusion(s32[256]{0:T(256)} %param.12, s32[]{:T(128)} %fusion.19), kind=kLoop, calls=%fused_computation.36 | loop fusion | flops 767 | bytes 1032 | tf_op jit(solution)/shard_map/reduce_sum | solution.py:60
  20.1 0.8 copy.15
  20.9 0.8 copy.16
  21.6 0.1 pad_maximum_fusion
  21.7 63.6 %all_gather.3 = f32[2048,32]{1,0:T(8,128)S(1)} all-gather(f32[32,32]{1,0:T(8,128)S(1)} %pad_maximum_fusion), channel_id=1, replica_groups=mesh['samp_0'=4,'samp_1'=8,'samp_2'=2,'gene'=4] {'samp_0','samp_1','samp..., dimensions={0}, use_global_device_ids=true | all-gather | bytes 266240 | tf_op jit(solution)/shard_map/all_gather | solution.py:15
  85.3 1.9 %fusion.15 = (f32[]{:T(128)}, bf16[16,2048,1]{0,1,2:T(8,128)(2,1)}, f32[16,2048]{0,1:T(8,128)S(1)}) fusion(f32[2048,32]{1,0:T(8,128)S(1)} %all_gather.3), kind=kLoop, calls=%fused_computation.19 | loop fusion | flops 163839 | bytes 458756 | tf_op jit(solution)/shard_map/reduce_sum | solution.py:96
  87.2 1.4 copy.21
  88.6 0.3 copy.17
  89.6 0.7 fusion.22
  90.3 0.8 dynamic-slice_multiply_fusion
  91.0 0.0 copy-done.1
  91.0 1.3 fusion.21
  92.3 0.0 all-to-all-done
  92.3 0.3 copy.19
  92.7 6.6 %multiply_convert_fusion.14 = bf16[16,2048,128]{1,2,0:T(8,128)(2,1)} fusion(f32[128]{0:T(128)S(1)} %dynamic-slice_multiply_fusion, s32[16]{0:T(128)S(1)} %iota_multiply_fusion, s32[2048,128]{0,1:T(8,128)S(1)} %copy.19, f32[16,2048]{1,0:T(8,128)S(1)} %copy.17), kind=kLoop, calls=%fused_computation.1.clone.clone.clone.clone.2 | loop fusion | flops 25165824 | bytes 9568832 | tf_op jit(solution)/shard_map/sbu,sbv->buv/dot_general | solution.py:39
  99.2 8.1 %fusion.12 = f32[128,128]{1,0:T(8,128)S(1)} fusion(bf16[16,2048,128]{1,2,0:T(8,128)(2,1)} %multiply_convert_fusion.14), kind=kOutput, calls=%fused_computation.15 | convolution fusion | flops 1073741824 | bytes 8454144 | tf_op jit(solution)/shard_map/sbu,sbv->buv/dot_general | solution.py:39
  107.3 1.4 gather_fusion
  108.8 1.9 %fusion.23 = (f32[]{:T(128)}, f32[1,128]{1,0:T(1,128)S(1)}) fusion(f32[128]{0:T(128)S(1)} %gather_fusion, f32[64,128]{1,0:T(8,128)} %bitcast.70, s32[]{:T(128)S(6)} %select_n.22, s32[]{:T(128)} %fusion.21, s32[]{:T(128)S(6)} %mul.117), kind=kLoop, calls=%fused_computation.40 | loop fusion | flops 767 | bytes 1552 | tf_op jit(solution)/shard_map/reduce_sum | solution.py:49
  110.7 0.7 fusion.17
  111.5 3.9 %multiply_reduce_fusion.1 = (f32[]{:T(128)}, f32[]{:T(128)}) fusion(f32[1,128]{1,0:T(1,128)S(1)} %get-tuple-element.5, bf16[16,2048,1]{1,2,0:T(2,128)(2,1)S(1)} %copy.21, f32[128]{0:T(128)S(1)} %dynamic-slice_multiply_fusion, s32[16]{0:T(128)S(1)} %iota_multiply_fusion, s32[2048,128]{0,1:T(8,128)S(1)} %copy.19, f32[16,2048]{1,0:T(8,128)S(1)} %copy.17), kind=kOutput, calls=%fused_computation.45 | convolution fusion | flops 33554944 | bytes 1246280 | tf_op jit(solution)/shard_map/dot_general | solution.py:93
  115.4 0.7 multiply_reduce_fusion
  116.1 3.3 %stack.23 = f32[5,1]{0,1:T(1,128)S(1)} concatenate(f32[1,1]{0,1:T(1,128)} %bitcast.10, f32[1,1]{0,1:T(1,128)} %bitcast.15, f32[1,1]{0,1:T(1,128)} %bitcast.16, f32[1,1]{0,1:T(1,128)} %bitcast.19, f32[1,1]{0,1:T(1,128)} %bitcast.20), dimensions={0} | concatenate | bytes 40 | tf_op jit(solution)/shard_map/stack | solution.py:52
  119.4 0.1 broadcast_multiply_fusion
  119.4 8.1 %psum.28 = f32[5,128]{1,0:T(8,128)S(1)} all-reduce(f32[5,128]{1,0:T(8,128)S(1)} %broadcast_multiply_fusion), channel_id=1, replica_groups=mesh['samp_0'=4,'samp_1'=8,'samp_2'=2,'gene'=4] {'samp_0'}, use_global_device_ids=true, to_apply=%region_8.9 | all-reduce | flops 640 | bytes 5120 | tf_op jit(solution)/shard_map/psum | solution.py:25
  127.5 11.4 %psum.29 = f32[5,128]{1,0:T(8,128)S(1)} all-reduce(f32[5,128]{1,0:T(8,128)S(1)} %psum.28), channel_id=1, replica_groups=mesh['samp_0'=4,'samp_1'=8,'samp_2'=2,'gene'=4] {'samp_1'}, use_global_device_ids=true, to_apply=%region_9.10 | all-reduce | flops 640 | bytes 5120 | tf_op jit(solution)/shard_map/psum | solution.py:25
  138.9 7.9 %psum.30 = f32[5,128]{1,0:T(8,128)S(1)} all-reduce(f32[5,128]{1,0:T(8,128)S(1)} %psum.29), channel_id=1, replica_groups=mesh['samp_0'=4,'samp_1'=8,'samp_2'=2,'gene'=4] {'samp_2'}, use_global_device_ids=true, to_apply=%region_10.11 | all-reduce | flops 640 | bytes 5120 | tf_op jit(solution)/shard_map/psum | solution.py:25
  146.8 8.4 %psum.31 = f32[5,128]{1,0:T(8,128)S(1)} all-reduce(f32[5,128]{1,0:T(8,128)S(1)} %psum.30), channel_id=1, replica_groups=mesh['samp_0'=4,'samp_1'=8,'samp_2'=2,'gene'=4] {'gene'}, use_global_device_ids=true, to_apply=%region_11.12 | all-reduce | flops 640 | bytes 5120 | tf_op jit(solution)/shard_map/psum | solution.py:25
  155.2 0.5 fusion.25
  (2 shorter events, 0.0 us)
Async XLA Ops:
  0.6 1.2 copy-start
  0.6 90.4 %copy-start.1 = (s32[128]{0:T(128)S(1)}, s32[128]{0:T(128)}, u32[]{:S(2)}) copy-start(s32[128]{0:T(128)} %param.13) | copy-start | bytes 1540
  3.0 89.3 %all-to-all-start = ((s32[32,64,128]{2,0,1:T(8,128)}), s32[32,64,128]{2,0,1:T(8,128)S(1)}, u32[]{:S(2)}, u32[]{:S(2)}) async-start(s32[32,64,128]{2,0,1:T(8,128)} %copy_bitcast_fusion), calls=%async_computation | async-start | bytes 2097152 | tf_op jit(solution)/shard_map/all_to_all | solution.py:83
where the time goes:
time: 157 us; the launch traced here: 156 us
  blocking collectives  99.4 us (63%)
  other arithmetic  17.8 us (11%)
  starting transfers between devices  13.1 us (8%)
  matrix products  12.7 us (8%)
  local copies, waits for them, and re-layouts  10.6 us (7%)
  between operations  2.05 us (1%)
    all_gather x1, blocking collectives, turned_gather(): result, at, done = (lax.all_gather(both, axis, axis=0, tiled=True), 0, [])  63.6 us
    psum x4, blocking collectives, by_axis(): array = lax.psum(array, axis)  35.8 us
    all_to_all x1, starting transfers between devices, local(): lax.all_to_all(genotypes, SAMP, split_axis=1, concat_axis=0, tiled=True)  13.1 us
    dot_general x1, matrix products, block_grams(): jnp.einsum('sbu,sbv->buv', stacked, stacked, preferred_element_type=jnp.f...  8.1 us
    dot_general x1, other arithmetic, block_grams(): jnp.einsum('sbu,sbv->buv', stacked, stacked, preferred_element_type=jnp.f...  6.58 us
    dot_general x1, matrix products, local(): jnp.dot(weighted_residual.reshape(1, -1), flattened, preferred_element_ty...  3.91 us
    another operation x1, local copies, waits for them, and re-layouts, block_stats(): return jnp.stack([burden_sum, burden_var, skat_sum, trace_one, trace_two])  3.27 us
  transfers between devices with their start and end apart: 1, of which 0 were waited for; matrix products, arithmetic and copies ran while one was open for 7% of the time, Pallas kernels for 0%

commit v1 on v0

v1 whole, which is shorter than its diff:
```python
import functools

import jax
import jax.numpy as jnp
from jax import lax
from jax.experimental import pallas as pl
from jax.experimental.pallas import tpu as pltpu
from jax.sharding import Mesh
from jax.sharding import PartitionSpec as P

BLK = 128
FIELDS = 16
MESH = pl.DeviceIdType.MESH
F32 = jnp.float32
BF16 = jnp.bfloat16
TAIL = 8


def total(x):
    return jnp.sum(jnp.sum(x, axis=1, keepdims=True), axis=0, keepdims=True)


def masked(words, k):
    if k == FIELDS - 1:
        words, k = jnp.right_shift(words, 2), k - 1
    return jnp.bitwise_and(words, 3 << (2 * k)).astype(F32)


def kernel(
    sizes, genotypes, freq, weight, residual, variant_weight, block_gene, gene_variants, out,
    staged, words, weights_in, residuals_in, rhs, lhs, scale, tail, part, gathered, freq_v, vw_v, bg_v, gv_v,
    rows_one, rows_two, out_v, stage_sem, small_sem, word_recv, word_send, side_recv, side_send,
    part_recv, part_send, one_recv, one_send, two_recv, two_send, out_sem,
):
    ny, nz, nc, nx = sizes
    rows = genotypes.shape[0]
    depth = ny * nc * rows
    genes_here = nz * nc // 2
    y, z, c, x = (lax.axis_index(a) for a in ("y", "z", "c", "x"))
    mine = y * nc + c

    stage = pltpu.make_async_copy(genotypes, staged, stage_sem)
    stage.start()
    smalls = [
        pltpu.make_async_copy(src, dst, small_sem.at[i])
        for i, (src, dst) in enumerate(
            ((freq, freq_v), (variant_weight, vw_v), (block_gene, bg_v), (gene_variants, gv_v))
        )
    ]
    for copy in smalls:
        copy.start()

    def near(dy, dc):
        return (lax.rem(y + dy, ny), z, lax.rem(c + dc, nc), x)

    def along(dz, dc):
        return (y, lax.rem(z + dz, nz), lax.rem(c + dc, nc), x)

    def across(dx, dy):
        return (lax.rem(y + dy, ny), z, c, lax.rem(x + dx, nx))

    order = sorted(range(1, ny), key=lambda d: -min(d, ny - d))
    near_peers = [(dy, dc) for dy in order + [0] for dc in range(nc) if (dy, dc) != (0, 0)]
    along_peers = [(dz, dc) for dz in range(nz) for dc in range(nc) if (dz, dc) != (0, 0)]
    across_peers = [(dx, dy) for dx in range(nx) for dy in range(ny) if (dx, dy) != (0, 0)]
    greeted = [near(*p) for p in near_peers]
    greeted += [along(*p) for p in along_peers if p[0] != 0]
    greeted += [across(*p) for p in across_peers if p[0] != 0]
    barrier = pltpu.get_barrier_semaphore()
    for peer in greeted:
        pl.semaphore_signal(barrier, inc=1, device_id=peer, device_id_type=MESH)
    pl.semaphore_wait(barrier, len(greeted))

    own_side = []
    for i, (src, dst) in enumerate(((weight, weights_in), (residual, residuals_in))):
        for peer in near_peers:
            pltpu.make_async_remote_copy(
                src_ref=src, dst_ref=dst.at[mine], send_sem=side_send.at[i], recv_sem=side_recv.at[i],
                device_id=near(*peer), device_id_type=MESH,
            ).start()
        copy = pltpu.make_async_copy(src, dst.at[mine], side_recv.at[i])
        copy.start()
        own_side.append(copy)

    def owner_of(j):
        distance = nz // 2 - (j + 1) // 2
        sign = 2 * (j % 2) - 1
        return lax.rem(z + sign * distance + nz, nz)

    stage.wait()

    def send_words(j, carry):
        zo = owner_of(j)
        for dy, dc in near_peers:
            to = near(dy, dc)
            column = pl.multiple_of(((to[0] * nz + zo) * nc + to[2]) * BLK, BLK)
            pltpu.make_async_remote_copy(
                src_ref=staged.at[:, pl.ds(column, BLK)], dst_ref=words.at[j, mine],
                send_sem=word_send, recv_sem=word_recv.at[j],
                device_id=to, device_id_type=MESH,
            ).start()
        column = pl.multiple_of(((y * nz + zo) * nc + c) * BLK, BLK)
        pltpu.make_async_copy(
            genotypes.at[:, pl.ds(column, BLK)], words.at[j, mine], word_recv.at[j]
        ).start()
        return carry

    lax.fori_loop(0, nz, send_words, 0)

    for i, dst in enumerate((weights_in, residuals_in)):
        pltpu.make_async_copy(dst, dst, side_recv.at[i]).wait()
    weight_all = jnp.concatenate([weights_in[g] for g in range(ny * nc)], axis=1)
    residual_all = jnp.concatenate([residuals_in[g] for g in range(ny * nc)], axis=1)
    rounded = weight_all.astype(BF16).astype(F32)
    cross = weight_all * residual_all
    high = cross.astype(BF16).astype(F32)
    low = (cross - high).astype(BF16).astype(F32)
    field = lax.broadcasted_iota(jnp.int32, (FIELDS, 1), 0)
    inverse = jnp.ones((FIELDS, 1), F32)
    for k in range(1, FIELDS):
        inverse = jnp.where(field == k, 0.25 ** min(k, FIELDS - 2), inverse)
    scale[...] = rounded * (inverse * inverse)
    extra = [a * inverse for a in (rounded, high, low)]
    row_id = lax.broadcasted_iota(jnp.int32, (2 * TAIL, depth), 0)
    for k in range(FIELDS):
        rows_k = jnp.zeros((2 * TAIL, depth), F32)
        for i, a in enumerate(extra):
            rows_k = jnp.where(row_id == i, a[k : k + 1], rows_k)
        lhs[BLK : BLK + 2 * TAIL, k * depth : (k + 1) * depth] = rows_k.astype(BF16)
    sums = (total(rounded), total(high + low), total(cross * residual_all))
    lane = lax.broadcasted_iota(jnp.int32, (TAIL, BLK), 1)
    sublane = lax.broadcasted_iota(jnp.int32, (TAIL, BLK), 0)
    tail_rows = jnp.zeros((TAIL, BLK), F32)
    for i, s in enumerate(sums):
        tail_rows = jnp.where(sublane == 3 + i, s, tail_rows)
    tail[...] = tail_rows

    def partial(j):
        pltpu.make_async_copy(words.at[j], words.at[j], word_recv.at[j]).wait()
        block = words[j].reshape(depth, BLK)
        turned = jnp.transpose(block)
        for k in range(FIELDS):
            rhs[k * depth : (k + 1) * depth, :] = masked(block, k).astype(BF16)
            lhs[:BLK, k * depth : (k + 1) * depth] = (masked(turned, k) * scale[k : k + 1, :]).astype(BF16)
        gram = jnp.dot(lhs[...], rhs[...], preferred_element_type=F32)
        part[j, :BLK] = gram[:BLK]
        part[j, BLK:] = gram[BLK : BLK + TAIL] + tail[...]

    def far_block(j, carry):
        partial(j)
        pltpu.make_async_remote_copy(
            src_ref=part.at[j], dst_ref=gathered.at[j], send_sem=part_send, recv_sem=part_recv,
            device_id=(y, owner_of(j), c, x), device_id_type=MESH,
        ).start()
        return carry

    lax.fori_loop(0, nz - 1, far_block, 0)
    partial(nz - 1)

    for copy in smalls:
        copy.wait()
    own = (y * nz + z) * nc + c
    doubled = 2.0 * freq_v[pl.ds(own, 1), :]
    own_block = x * (ny * nz * nc) + own
    bg = bg_v[...]
    block_id = lax.broadcasted_iota(jnp.int32, bg.shape, 0) * BLK + lax.broadcasted_iota(jnp.int32, bg.shape, 1)
    gene = total(jnp.where(block_id == own_block, bg, 0))
    first = total((bg < gene).astype(jnp.int32))
    row_lane = lax.broadcasted_iota(jnp.int32, (1, BLK), 1)
    counted = total(jnp.where(row_lane == gene, gv_v[...], 0))
    live = (own_block - first) * BLK + row_lane < counted
    effective = jnp.where(live, vw_v[pl.ds(own, 1), :], 0.0)

    pltpu.make_async_copy(gathered, gathered, part_recv).wait()
    summed = part[nz - 1]
    for j in range(nz - 1):
        summed = summed + gathered[j]
    raw = summed[:BLK]
    linear = summed[BLK : BLK + 1]
    weight_sum = summed[BLK + 3 : BLK + 4]
    score = summed[BLK + 1 : BLK + 2] + summed[BLK + 2 : BLK + 3] - doubled * summed[BLK + 4 : BLK + 5]
    down = lax.broadcasted_iota(jnp.int32, (BLK, BLK), 0)
    side = lax.broadcasted_iota(jnp.int32, (BLK, BLK), 1)
    stacked = jnp.where(down == 0, doubled, jnp.where(down == 1, linear, jnp.where(down == 2, effective, 0.0)))
    upright = jnp.transpose(stacked)
    doubled_c, linear_c, effective_c = upright[:, 0:1], upright[:, 1:2], upright[:, 2:3]
    gram = raw - doubled_c * (linear - doubled * weight_sum) - linear_c * doubled
    scaled = effective_c * gram * effective
    weighted_score = effective * score
    stats = (
        total(weighted_score),
        total(scaled),
        total(weighted_score * weighted_score),
        total(jnp.where(down == side, scaled, 0.0)),
        total(scaled * scaled),
    )
    near_gene = gene - (x * ny + y) * genes_here
    row = jnp.zeros((1, BLK), F32)
    for i, s in enumerate(stats):
        row = jnp.where(row_lane == i * genes_here + near_gene, s, row)
    at_variance = len(stats) * genes_here
    share = jnp.where(c == 0, tail[5:6, :], 0.0)
    row = jnp.where(row_lane == at_variance, share, row)
    seat = z * nc + c
    rows_one[seat] = row
    for peer in along_peers:
        pltpu.make_async_remote_copy(
            src_ref=rows_one.at[seat], dst_ref=rows_one.at[seat], send_sem=one_send, recv_sem=one_recv,
            device_id=along(*peer), device_id_type=MESH,
        ).start()
    count = nz * nc - 1
    pltpu.make_async_copy(rows_one.at[pl.ds(0, count)], rows_one.at[pl.ds(0, count)], one_recv).wait()
    genes = rows_one[0]
    for i in range(1, count + 1):
        genes = genes + rows_one[i]

    place = x * ny + y
    samples = depth * nz * FIELDS
    variance = total(jnp.where(row_lane == at_variance, genes, 0.0)) / samples
    totals = [
        pltpu.roll(genes, lax.rem(place * genes_here - i * genes_here + BLK, BLK), 1)
        for i in range(len(stats))
    ]
    here = jnp.logical_and(row_lane >= place * genes_here, row_lane < (place + 1) * genes_here)
    totals = [jnp.where(here, t, 1.0) for t in totals]
    burden = totals[0] / jnp.sqrt(variance * totals[1])
    skat = (totals[2] - variance * totals[3]) / (variance * jnp.sqrt(2.0 * totals[4]))
    pair_row = lax.broadcasted_iota(jnp.int32, (2, BLK), 0)
    rows_two[place] = jnp.where(here, jnp.where(pair_row == 0, burden, skat), 0.0)
    for peer in across_peers:
        pltpu.make_async_remote_copy(
            src_ref=rows_two.at[place], dst_ref=rows_two.at[place], send_sem=two_send, recv_sem=two_recv,
            device_id=across(*peer), device_id_type=MESH,
        ).start()
    count = nx * ny - 1
    pltpu.make_async_copy(rows_two.at[pl.ds(0, count)], rows_two.at[pl.ds(0, count)], two_recv).wait()
    scores = rows_two[0]
    for i in range(1, count + 1):
        scores = scores + rows_two[i]
    out[...] = scores

    sent = len(near_peers)
    for i, dst in enumerate((weights_in, residuals_in)):
        pltpu.make_async_copy(dst.at[pl.ds(0, sent)], dst.at[pl.ds(0, sent)], side_send.at[i]).wait()
    span = words.at[:, pl.ds(0, sent)]
    pltpu.make_async_copy(span, span, word_send).wait()
    pltpu.make_async_copy(gathered, gathered, part_send).wait()
    span = rows_one.at[pl.ds(0, len(along_peers))]
    pltpu.make_async_copy(span, span, one_send).wait()
    span = rows_two.at[pl.ds(0, len(across_peers))]
    pltpu.make_async_copy(span, span, two_send).wait()


def local(
    sizes, genotypes, allele_freq, sample_weight, residual, variant_weight, block_gene, gene_variants
):
    ny, nz, nc, nx = sizes
    rows, columns = genotypes.shape
    group = ny * nc
    depth = group * rows
    blocks = columns // BLK
    args = (
        genotypes,
        allele_freq.reshape(blocks, BLK),
        sample_weight,
        residual,
        variant_weight.reshape(blocks, BLK),
        block_gene.reshape(-1, BLK),
        gene_variants.reshape(1, -1),
    )
    anywhere = pl.BlockSpec(memory_space=pl.ANY)
    dma = pltpu.SemaphoreType.DMA
    scores = pl.pallas_call(
        functools.partial(kernel, sizes),
        out_shape=jax.ShapeDtypeStruct((2, BLK), F32),
        in_specs=[anywhere] * len(args),
        out_specs=pl.BlockSpec(memory_space=pltpu.VMEM),
        scratch_shapes=[
            pltpu.VMEM((rows, columns), jnp.int32),
            pltpu.VMEM((nz, group, rows, BLK), jnp.int32),
            pltpu.VMEM((group, FIELDS, rows), F32),
            pltpu.VMEM((group, FIELDS, rows), F32),
            pltpu.VMEM((FIELDS * depth, BLK), BF16),
            pltpu.VMEM((BLK + 2 * TAIL, FIELDS * depth), BF16),
            pltpu.VMEM((FIELDS, depth), F32),
            pltpu.VMEM((TAIL, BLK), F32),
            pltpu.VMEM((nz, BLK + TAIL, BLK), F32),
            pltpu.VMEM((nz - 1, BLK + TAIL, BLK), F32),
            pltpu.VMEM(args[1].shape, F32),
            pltpu.VMEM(args[4].shape, F32),
            pltpu.VMEM(args[5].shape, jnp.int32),
            pltpu.VMEM(args[6].shape, jnp.int32),
            pltpu.VMEM((nz * nc, 1, BLK), F32),
            pltpu.VMEM((nx * ny, 2, BLK), F32),
            pltpu.VMEM((2, BLK), F32),
            dma, dma((4,)), dma((nz,)), dma, dma((2,)), dma((2,)),
            dma, dma, dma, dma, dma, dma, dma,
        ],
        compiler_params=pltpu.CompilerParams(collective_id=0, has_side_effects=True),
    )(*args)
    return (scores[0], scores[1])


def solution(mesh):
    nx = mesh.shape["gene"]
    sizes = (4, 8, 2, nx)
    torus = Mesh(mesh.devices.reshape(sizes), ("y", "z", "c", "x"))
    samp = ("y", "z", "c")
    placed = (P(samp, "x"), P("x"), P(None, samp), P(None, samp), P("x"), P(), P())
    step = functools.partial(local, sizes)
    return jax.shard_map(step, mesh=torus, in_specs=placed, out_specs=(P(), P()), check_vma=False)
```

time: 157 us -> 44.1 us (0.28)
  blocking collectives: 99.4 us -> 0 us
  Pallas kernels: 0 us -> 42.1 us
  other arithmetic: 17.8 us -> 0 us
  starting transfers between devices: 13.1 us -> 0 us
  matrix products: 12.7 us -> 0 us
  local copies, waits for them, and re-layouts: 10.6 us -> 1.25 us
    all_gather x1 -> x0, blocking collectives: 63.6 us -> none  [turned_gather(): result, at, done = (lax.all_gather(both, axis, axis=0, tiled=True), 0, [])]
    pallas_call x0 -> x1, Pallas kernels: none -> 42.1 us  [local(): pl.pallas_call(functools.partial(kernel, sizes), out_shape=jax.ShapeDtype...]
    psum x4 -> x0, blocking collectives: 35.8 us -> none  [by_axis(): array = lax.psum(array, axis)]
    all_to_all x1 -> x0, starting transfers between devices: 13.1 us -> none  [local(): lax.all_to_all(genotypes, SAMP, split_axis=1, concat_axis=0, tiled=True)]
    dot_general x3 -> x0, matrix products: 12.7 us -> none  [the longest x1 8.1 us: block_grams(): jnp.einsum('sbu,sbv->buv', stacked, stacked, preferred_element_type=jnp.f...]
    reduce_sum x6 -> x0, other arithmetic: 9.12 us -> none  [the longest x1 1.96 us: live_weights(): jnp.sum((block_gene[None, :] < gene_of[:, None]).astype(jnp.int32), axis=1)]
    dot_general x2 -> x0, other arithmetic: 6.65 us -> none  [the longest x1 6.58 us: block_grams(): jnp.einsum('sbu,sbv->buv', stacked, stacked, preferred_element_type=jnp.f...]
    another operation x1 -> x0, local copies, waits for them, and re-layouts: 3.27 us -> none  [block_stats(): return jnp.stack([burden_sum, burden_var, skat_sum, trace_one, trace_two])]
  transfers between devices with their start and end apart: 1 -> 0, of which waited for: 0 -> 0; matrix products, arithmetic and copies ran while one was open for 7% -> 0% of each run, Pallas kernels for 0% -> 0%
where the time goes in v1:
time: 44.1 us; the launch traced here: 44 us
  Pallas kernels  42.1 us (95%)
  local copies, waits for them, and re-layouts  1.25 us (3%)
  between operations  0.64 us (1%)
    pallas_call x1, Pallas kernels, local(): pl.pallas_call(functools.partial(kernel, sizes), out_shape=jax.ShapeDtype...  42.1 us
    squeeze x1, local copies, waits for them, and re-layouts, local(): return (scores[0], scores[1])  1.25 us

profile of v1, /device:TPU:1, one launch (start us, length us, event | category | flops | bytes accessed | tf_op | source)
XLA Modules:
  0.0 44.0 jit_solution(4801443654725521642)
XLA Ops:
  0.6 42.1 %shard_map.86 = f32[2,128]{1,0:T(2,128)} custom-call(s32[32,8192]{1,0:T(8,128)} %genotypes.1, f32[64,128]{1,0:T(8,128)} %bitcast.8, f32[16,32]{1,0:T(8,128)} %weight.1, f32[16,32]{1,0:T(8,128)} %residual.1, f32[64,128]{1,0:T(8,128)} %bitcast.9, s32[2,128]{1,0:T(2,128)} %bitcast.10, s32[1,128]{1,0:T(1,128)} %bitcast.11), custom_call_target="tpu_custom_call" | custom-call | tf_op jit(solution)/shard_map/pallas_call | solution.py:273
  42.8 1.3 %slice_bitcast_fusion = (f32[128]{0:T(128)}, f32[128]{0:T(128)}) fusion(f32[2,128]{1,0:T(2,128)} %shard_map.86), kind=kLoop, calls=%fused_computation | loop fusion | bytes 2048 | tf_op jit(solution)/shard_map/squeeze | solution.py:301

commit v2 on v1

--- a/solution.py
+++ b/solution.py
@@ -9,6 +9,7 @@
 from jax.sharding import PartitionSpec as P
 
 BLK = 128
+HALF = BLK // 2
 FIELDS = 16
 MESH = pl.DeviceIdType.MESH
 F32 = jnp.float32
@@ -29,8 +30,8 @@
 def kernel(
     sizes, genotypes, freq, weight, residual, variant_weight, block_gene, gene_variants, out,
     staged, words, weights_in, residuals_in, rhs, lhs, scale, tail, part, gathered, freq_v, vw_v, bg_v, gv_v,
-    rows_one, rows_two, out_v, stage_sem, small_sem, word_recv, word_send, side_recv, side_send,
-    part_recv, part_send, one_recv, one_send, two_recv, two_send, out_sem,
+    rows_one, rows_two, stage_sem, small_sem, word_recv, word_send, side_recv, side_send,
+    part_recv, part_send, one_recv, one_send, two_recv, two_send,
 ):
     ny, nz, nc, nx = sizes
     rows = genotypes.shape[0]
@@ -134,6 +135,9 @@
     for i, s in enumerate(sums):
         tail_rows = jnp.where(sublane == 3 + i, s, tail_rows)
     tail[...] = tail_rows
+    fold_down = lax.broadcasted_iota(jnp.int32, (HALF, BLK), 0)
+    fold_side = lax.broadcasted_iota(jnp.int32, (HALF, BLK), 1)
+    folded = jnp.logical_and(fold_side >= HALF, fold_down >= fold_side - HALF)
 
     def partial(j):
         pltpu.make_async_copy(words.at[j], words.at[j], word_recv.at[j]).wait()
@@ -143,8 +147,10 @@
             rhs[k * depth : (k + 1) * depth, :] = masked(block, k).astype(BF16)
             lhs[:BLK, k * depth : (k + 1) * depth] = (masked(turned, k) * scale[k : k + 1, :]).astype(BF16)
         gram = jnp.dot(lhs[...], rhs[...], preferred_element_type=F32)
-        part[j, :BLK] = gram[:BLK]
-        part[j, BLK:] = gram[BLK : BLK + TAIL] + tail[...]
+        low_rows = gram[HALF:BLK]
+        part[j, :HALF] = jnp.where(folded, pltpu.roll(gram[:HALF], HALF, 1), low_rows)
+        corner = jnp.sum(jnp.where(fold_side - HALF == fold_down, low_rows, 0.0), axis=0, keepdims=True)
+        part[j, HALF:] = gram[BLK : BLK + TAIL] + jnp.where(sublane == 6, corner, tail[...])
 
     def far_block(j, carry):
         partial(j)
@@ -175,24 +181,33 @@
     summed = part[nz - 1]
     for j in range(nz - 1):
         summed = summed + gathered[j]
-    raw = summed[:BLK]
-    linear = summed[BLK : BLK + 1]
-    weight_sum = summed[BLK + 3 : BLK + 4]
-    score = summed[BLK + 1 : BLK + 2] + summed[BLK + 2 : BLK + 3] - doubled * summed[BLK + 4 : BLK + 5]
+    ends = summed[HALF:]
+    linear, weight_sum = ends[0:1], ends[3:4]
+    score = ends[1:2] + ends[2:3] - doubled * ends[4:5]
     down = lax.broadcasted_iota(jnp.int32, (BLK, BLK), 0)
-    side = lax.broadcasted_iota(jnp.int32, (BLK, BLK), 1)
     stacked = jnp.where(down == 0, doubled, jnp.where(down == 1, linear, jnp.where(down == 2, effective, 0.0)))
     upright = jnp.transpose(stacked)
-    doubled_c, linear_c, effective_c = upright[:, 0:1], upright[:, 1:2], upright[:, 2:3]
-    gram = raw - doubled_c * (linear - doubled * weight_sum) - linear_c * doubled
-    scaled = effective_c * gram * effective
+
+    def by_row(i):
+        return jnp.where(folded, upright[:HALF, i : i + 1], upright[HALF:, i : i + 1])
+
+    def by_lane(row):
+        return jnp.where(folded, pltpu.roll(row, HALF, 1), row)
+
+    doubled_v, linear_v = by_lane(doubled), by_lane(linear)
+    gram = summed[:HALF] - by_row(0) * (linear_v - doubled_v * weight_sum) - by_row(1) * doubled_v
+    scaled = by_row(2) * gram * by_lane(effective)
+    first_diagonal = fold_side - HALF == fold_down
+    twice = jnp.where(first_diagonal, 1.0, 2.0) * scaled
+    corner = ends[6:7] - doubled * (2.0 * linear - doubled * weight_sum)
+    corner = jnp.where(row_lane >= HALF, effective * effective * corner, 0.0)
     weighted_score = effective * score
     stats = (
         total(weighted_score),
-        total(scaled),
+        total(twice) + total(corner),
         total(weighted_score * weighted_score),
-        total(jnp.where(down == side, scaled, 0.0)),
-        total(scaled * scaled),
+        total(jnp.where(first_diagonal, scaled, 0.0)) + total(corner),
+        total(twice * scaled) + total(corner * corner),
     )
     near_gene = gene - (x * ny + y) * genes_here
     row = jnp.zeros((1, BLK), F32)
@@ -272,7 +287,7 @@
     dma = pltpu.SemaphoreType.DMA
     scores = pl.pallas_call(
         functools.partial(kernel, sizes),
-        out_shape=jax.ShapeDtypeStruct((2, BLK), F32),
+        out_shape=pltpu.VMEM((2, BLK), F32),
         in_specs=[anywhere] * len(args),
         out_specs=pl.BlockSpec(memory_space=pltpu.VMEM),
         scratch_shapes=[
@@ -284,17 +299,16 @@
             pltpu.VMEM((BLK + 2 * TAIL, FIELDS * depth), BF16),
             pltpu.VMEM((FIELDS, depth), F32),
             pltpu.VMEM((TAIL, BLK), F32),
-            pltpu.VMEM((nz, BLK + TAIL, BLK), F32),
-            pltpu.VMEM((nz - 1, BLK + TAIL, BLK), F32),
+            pltpu.VMEM((nz, HALF + TAIL, BLK), F32),
+            pltpu.VMEM((nz - 1, HALF + TAIL, BLK), F32),
             pltpu.VMEM(args[1].shape, F32),
             pltpu.VMEM(args[4].shape, F32),
             pltpu.VMEM(args[5].shape, jnp.int32),
             pltpu.VMEM(args[6].shape, jnp.int32),
             pltpu.VMEM((nz * nc, 1, BLK), F32),
             pltpu.VMEM((nx * ny, 2, BLK), F32),
-            pltpu.VMEM((2, BLK), F32),
             dma, dma((4,)), dma((nz,)), dma, dma((2,)), dma((2,)),
-            dma, dma, dma, dma, dma, dma, dma,
+            dma, dma, dma, dma, dma, dma,
         ],
         compiler_params=pltpu.CompilerParams(collective_id=0, has_side_effects=True),
     )(*args)

time: 44.1 us -> 38.7 us (0.88)
  Pallas kernels: 42.1 us -> 37.4 us
  local copies, waits for them, and re-layouts: 1.25 us -> 0.52 us
    pallas_call x1, Pallas kernels: 42.1 us -> 37.4 us  [local(): pl.pallas_call(functools.partial(kernel, sizes), out_shape=pltpu.VMEM((2,...]
    squeeze x1, local copies, waits for them, and re-layouts: 1.25 us -> 0.52 us  [local(): return (scores[0], scores[1])]
where the time goes in v2:
time: 38.7 us; the launch traced here: 38.6 us
  Pallas kernels  37.4 us (97%)
  between operations  0.64 us (2%)
  local copies, waits for them, and re-layouts  0.52 us (1%)
    pallas_call x1, Pallas kernels, local(): pl.pallas_call(functools.partial(kernel, sizes), out_shape=pltpu.VMEM((2,...  37.4 us

profile of v2, /device:TPU:1, one launch (start us, length us, event | category | flops | bytes accessed | tf_op | source)
XLA Modules:
  0.0 38.6 jit_solution(10048965434037861227)
XLA Ops:
  0.6 37.4 %shard_map.86 = f32[2,128]{1,0:T(2,128)S(1)} custom-call(s32[32,8192]{1,0:T(8,128)} %genotypes.1, f32[64,128]{1,0:T(8,128)} %bitcast.8, f32[16,32]{1,0:T(8,128)} %weight.1, f32[16,32]{1,0:T(8,128)} %residual.1, f32[64,128]{1,0:T(8,128)} %bitcast.9, s32[2,128]{1,0:T(2,128)} %bitcast.10, s32[1,128]{1,0:T(1,128)} %bitcast.11), custom_call_target="tpu_custom_call" | custom-call | tf_op jit(solution)/shard_map/pallas_call | solution.py:288
  38.1 0.5 %slice_bitcast_fusion = (f32[128]{0:T(128)}, f32[128]{0:T(128)}) fusion(f32[2,128]{1,0:T(2,128)S(1)} %shard_map.86), kind=kLoop, calls=%fused_computation | loop fusion | bytes 2048 | tf_op jit(solution)/shard_map/squeeze | solution.py:315

commit v3 on v2

--- a/solution.py
+++ b/solution.py
@@ -29,8 +29,8 @@
 
 def kernel(
     sizes, genotypes, freq, weight, residual, variant_weight, block_gene, gene_variants, out,
-    staged, words, weights_in, residuals_in, rhs, lhs, scale, tail, part, gathered, freq_v, vw_v, bg_v, gv_v,
-    rows_one, rows_two, stage_sem, small_sem, word_recv, word_send, side_recv, side_send,
+    staged, words, side_staged, side_in, rhs, lhs, scale, tail, part, gathered, freq_v, vw_v, bg_v, gv_v,
+    rows_one, rows_two, stage_sem, side_sem, small_sem, word_recv, word_send, side_recv, side_send,
     part_recv, part_send, one_recv, one_send, two_recv, two_send,
 ):
     ny, nz, nc, nx = sizes
@@ -40,6 +40,12 @@
     y, z, c, x = (lax.axis_index(a) for a in ("y", "z", "c", "x"))
     mine = y * nc + c
 
+    side_copies = [
+        pltpu.make_async_copy(src, side_staged.at[i], side_sem.at[i])
+        for i, src in enumerate((weight, residual))
+    ]
+    for copy in side_copies:
+        copy.start()
     stage = pltpu.make_async_copy(genotypes, staged, stage_sem)
     stage.start()
     smalls = [
@@ -72,35 +78,33 @@
         pl.semaphore_signal(barrier, inc=1, device_id=peer, device_id_type=MESH)
     pl.semaphore_wait(barrier, len(greeted))
 
-    own_side = []
-    for i, (src, dst) in enumerate(((weight, weights_in), (residual, residuals_in))):
-        for peer in near_peers:
-            pltpu.make_async_remote_copy(
-                src_ref=src, dst_ref=dst.at[mine], send_sem=side_send.at[i], recv_sem=side_recv.at[i],
-                device_id=near(*peer), device_id_type=MESH,
-            ).start()
-        copy = pltpu.make_async_copy(src, dst.at[mine], side_recv.at[i])
-        copy.start()
-        own_side.append(copy)
-
-    def owner_of(j):
+    for copy in side_copies:
+        copy.wait()
+    for peer in near_peers:
+        pltpu.make_async_remote_copy(
+            src_ref=side_staged, dst_ref=side_in.at[mine], send_sem=side_send, recv_sem=side_recv,
+            device_id=near(*peer), device_id_type=MESH,
+        ).start()
+    for i, src in enumerate((weight, residual)):
+        pltpu.make_async_copy(src, side_in.at[mine, i], side_recv).start()
+
+    def owner_of(j, core):
         distance = nz // 2 - (j + 1) // 2
-        sign = 2 * (j % 2) - 1
+        sign = (2 * (j % 2) - 1) * (1 - 2 * core)
         return lax.rem(z + sign * distance + nz, nz)
 
     stage.wait()
 
     def send_words(j, carry):
-        zo = owner_of(j)
         for dy, dc in near_peers:
             to = near(dy, dc)
-            column = pl.multiple_of(((to[0] * nz + zo) * nc + to[2]) * BLK, BLK)
+            column = pl.multiple_of(((to[0] * nz + owner_of(j, to[2])) * nc + to[2]) * BLK, BLK)
             pltpu.make_async_remote_copy(
                 src_ref=staged.at[:, pl.ds(column, BLK)], dst_ref=words.at[j, mine],
                 send_sem=word_send, recv_sem=word_recv.at[j],
                 device_id=to, device_id_type=MESH,
             ).start()
-        column = pl.multiple_of(((y * nz + zo) * nc + c) * BLK, BLK)
+        column = pl.multiple_of(((y * nz + owner_of(j, c)) * nc + c) * BLK, BLK)
         pltpu.make_async_copy(
             genotypes.at[:, pl.ds(column, BLK)], words.at[j, mine], word_recv.at[j]
         ).start()
@@ -108,10 +112,10 @@
 
     lax.fori_loop(0, nz, send_words, 0)
 
-    for i, dst in enumerate((weights_in, residuals_in)):
-        pltpu.make_async_copy(dst, dst, side_recv.at[i]).wait()
-    weight_all = jnp.concatenate([weights_in[g] for g in range(ny * nc)], axis=1)
-    residual_all = jnp.concatenate([residuals_in[g] for g in range(ny * nc)], axis=1)
+    pltpu.make_async_copy(side_in, side_in, side_recv).wait()
+    weight_all, residual_all = (
+        jnp.concatenate([side_in[g, i] for g in range(ny * nc)], axis=1) for i in range(2)
+    )
     rounded = weight_all.astype(BF16).astype(F32)
     cross = weight_all * residual_all
     high = cross.astype(BF16).astype(F32)
@@ -156,7 +160,7 @@
         partial(j)
         pltpu.make_async_remote_copy(
             src_ref=part.at[j], dst_ref=gathered.at[j], send_sem=part_send, recv_sem=part_recv,
-            device_id=(y, owner_of(j), c, x), device_id_type=MESH,
+            device_id=(y, owner_of(j, c), c, x), device_id_type=MESH,
         ).start()
         return carry
 
@@ -255,8 +259,8 @@
     out[...] = scores
 
     sent = len(near_peers)
-    for i, dst in enumerate((weights_in, residuals_in)):
-        pltpu.make_async_copy(dst.at[pl.ds(0, sent)], dst.at[pl.ds(0, sent)], side_send.at[i]).wait()
+    span = side_in.at[pl.ds(0, sent)]
+    pltpu.make_async_copy(span, span, side_send).wait()
     span = words.at[:, pl.ds(0, sent)]
     pltpu.make_async_copy(span, span, word_send).wait()
     pltpu.make_async_copy(gathered, gathered, part_send).wait()
@@ -293,8 +297,8 @@
         scratch_shapes=[
             pltpu.VMEM((rows, columns), jnp.int32),
             pltpu.VMEM((nz, group, rows, BLK), jnp.int32),
-            pltpu.VMEM((group, FIELDS, rows), F32),
-            pltpu.VMEM((group, FIELDS, rows), F32),
+            pltpu.VMEM((2, FIELDS, rows), F32),
+            pltpu.VMEM((group, 2, FIELDS, rows), F32),
             pltpu.VMEM((FIELDS * depth, BLK), BF16),
             pltpu.VMEM((BLK + 2 * TAIL, FIELDS * depth), BF16),
             pltpu.VMEM((FIELDS, depth), F32),
@@ -307,7 +311,7 @@
             pltpu.VMEM(args[6].shape, jnp.int32),
             pltpu.VMEM((nz * nc, 1, BLK), F32),
             pltpu.VMEM((nx * ny, 2, BLK), F32),
-            dma, dma((4,)), dma((nz,)), dma, dma((2,)), dma((2,)),
+            dma, dma((2,)), dma((4,)), dma((nz,)), dma, dma, dma,
             dma, dma, dma, dma, dma, dma,
         ],
         compiler_params=pltpu.CompilerParams(collective_id=0, has_side_effects=True),

time: 38.7 us -> 38.2 us (0.987)
  Pallas kernels: 37.4 us -> 37 us
    pallas_call x1, Pallas kernels: 37.4 us -> 37 us  [local(): pl.pallas_call(functools.partial(kernel, sizes), out_shape=pltpu.VMEM((2,...]
where the time goes in v3:
time: 38.2 us; the launch traced here: 38.1 us
  Pallas kernels  37 us (97%)
  between operations  0.64 us (2%)
  local copies, waits for them, and re-layouts  0.52 us (1%)
    pallas_call x1, Pallas kernels, local(): pl.pallas_call(functools.partial(kernel, sizes), out_shape=pltpu.VMEM((2,...  37 us

profile of v3, /device:TPU:1, one launch (start us, length us, event | category | flops | bytes accessed | tf_op | source)
XLA Modules:
  0.0 38.1 jit_solution(5483523965969554786)
XLA Ops:
  0.6 37.0 %shard_map.86 = f32[2,128]{1,0:T(2,128)S(1)} custom-call(s32[32,8192]{1,0:T(8,128)} %genotypes.1, f32[64,128]{1,0:T(8,128)} %bitcast.8, f32[16,32]{1,0:T(8,128)} %weight.1, f32[16,32]{1,0:T(8,128)} %residual.1, f32[64,128]{1,0:T(8,128)} %bitcast.9, s32[2,128]{1,0:T(2,128)} %bitcast.10, s32[1,128]{1,0:T(1,128)} %bitcast.11), custom_call_target="tpu_custom_call" | custom-call | tf_op jit(solution)/shard_map/pallas_call | solution.py:292
  37.6 0.5 %slice_bitcast_fusion = (f32[128]{0:T(128)}, f32[128]{0:T(128)}) fusion(f32[2,128]{1,0:T(2,128)S(1)} %shard_map.86), kind=kLoop, calls=%fused_computation | loop fusion | bytes 2048 | tf_op jit(solution)/shard_map/squeeze | solution.py:319

commit v4 on v3

--- a/solution.py
+++ b/solution.py
@@ -1,4 +1,5 @@
 import functools
+import itertools
 
 import jax
 import jax.numpy as jnp
@@ -30,8 +31,8 @@
 def kernel(
     sizes, genotypes, freq, weight, residual, variant_weight, block_gene, gene_variants, out,
     staged, words, side_staged, side_in, rhs, lhs, scale, tail, part, gathered, freq_v, vw_v, bg_v, gv_v,
-    rows_one, rows_two, stage_sem, side_sem, small_sem, word_recv, word_send, side_recv, side_send,
-    part_recv, part_send, one_recv, one_send, two_recv, two_send,
+    rows_one, rows_two, rows_all, stage_sem, side_sem, small_sem, word_recv, word_send, side_recv, side_send,
+    part_recv, part_send, one_recv, one_send, two_recv, two_send, row_recv, row_send,
 ):
     ny, nz, nc, nx = sizes
     rows = genotypes.shape[0]
@@ -60,23 +61,44 @@
     def near(dy, dc):
         return (lax.rem(y + dy, ny), z, lax.rem(c + dc, nc), x)
 
-    def along(dz, dc):
-        return (y, lax.rem(z + dz, nz), lax.rem(c + dc, nc), x)
-
-    def across(dx, dy):
-        return (lax.rem(y + dy, ny), z, c, lax.rem(x + dx, nx))
-
+    def along(dz, core):
+        return (y, lax.rem(z + dz, nz), core, x)
+
+    def across(dx, dy, core):
+        return (lax.rem(y + dy, ny), z, core, lax.rem(x + dx, nx))
+
+    head = nc - 1
     order = sorted(range(1, ny), key=lambda d: -min(d, ny - d))
     near_peers = [(dy, dc) for dy in order + [0] for dc in range(nc) if (dy, dc) != (0, 0)]
-    along_peers = [(dz, dc) for dz in range(nz) for dc in range(nc) if (dz, dc) != (0, 0)]
-    across_peers = [(dx, dy) for dx in range(nx) for dy in range(ny) if (dx, dy) != (0, 0)]
-    greeted = [near(*p) for p in near_peers]
-    greeted += [along(*p) for p in along_peers if p[0] != 0]
-    greeted += [across(*p) for p in across_peers if p[0] != 0]
+    far_x = [(dx, dy) for dx in range(1, nx) for dy in range(ny)]
     barrier = pltpu.get_barrier_semaphore()
-    for peer in greeted:
-        pl.semaphore_signal(barrier, inc=1, device_id=peer, device_id_type=MESH)
-    pl.semaphore_wait(barrier, len(greeted))
+
+    def greet(peers):
+        for peer in peers:
+            pl.semaphore_signal(barrier, inc=1, device_id=peer, device_id_type=MESH)
+
+    greet([near(*p) for p in near_peers])
+    greet([along(dz, c) for dz in range(1, nz)])
+    greet([across(*p, head) for p in far_x])
+
+    @pl.when(c == head)
+    def _():
+        greet([along(dz, core) for dz in range(1, nz) for core in range(nc) if core != head])
+
+    is_first = jnp.logical_and(x + y + z == 0, c == head)
+
+    def known(y, z, c, x):
+        return (x == 0) & ((z == 0) | (y == 0)) | (z == 0) & (c == head)
+
+    @pl.when(is_first)
+    def _():
+        for to in itertools.product(range(ny), range(nz), range(nc), range(nx)):
+            if not known(*to):
+                greet([to])
+
+    at_head = len(near_peers) + nz - 1 + len(far_x) * nc
+    elsewhere = len(near_peers) + (nz - 1) * 2
+    pl.semaphore_wait(barrier, jnp.where(c == head, at_head, elsewhere) + jnp.where(known(y, z, c, x), 0, 1))
 
     for copy in side_copies:
         copy.wait()
@@ -88,9 +110,13 @@
     for i, src in enumerate((weight, residual)):
         pltpu.make_async_copy(src, side_in.at[mine, i], side_recv).start()
 
+    def outward(core):
+        middle = nz // 2
+        return jnp.where(z < middle, 1, jnp.where(z > middle, -1, 1 - 2 * core))
+
     def owner_of(j, core):
         distance = nz // 2 - (j + 1) // 2
-        sign = (2 * (j % 2) - 1) * (1 - 2 * core)
+        sign = (2 * (j % 2) - 1) * outward(core)
         return lax.rem(z + sign * distance + nz, nz)
 
     stage.wait()
@@ -158,9 +184,10 @@
 
     def far_block(j, carry):
         partial(j)
+        owner = owner_of(j, c)
         pltpu.make_async_remote_copy(
-            src_ref=part.at[j], dst_ref=gathered.at[j], send_sem=part_send, recv_sem=part_recv,
-            device_id=(y, owner_of(j, c), c, x), device_id_type=MESH,
+            src_ref=part.at[j], dst_ref=gathered.at[lax.rem(owner - z + nz, nz) - 1], send_sem=part_send, recv_sem=part_recv,
+            device_id=(y, owner, c, x), device_id_type=MESH,
         ).start()
         return carry
 
@@ -221,42 +248,120 @@
     share = jnp.where(c == 0, tail[5:6, :], 0.0)
     row = jnp.where(row_lane == at_variance, share, row)
     seat = z * nc + c
+    place = x * ny + y
+    group = nz * nc
+    places = nx * ny
+    samples = depth * nz * FIELDS
     rows_one[seat] = row
-    for peer in along_peers:
+
+    @pl.when(place != 0)
+    def _():
+        pltpu.make_async_remote_copy(
+            src_ref=rows_one.at[seat], dst_ref=rows_all.at[place * group + seat], send_sem=row_send, recv_sem=row_recv,
+            device_id=(0, 0, head, 0), device_id_type=MESH,
+        ).start()
+
+    def send_row(dz):
         pltpu.make_async_remote_copy(
             src_ref=rows_one.at[seat], dst_ref=rows_one.at[seat], send_sem=one_send, recv_sem=one_recv,
-            device_id=along(*peer), device_id_type=MESH,
+            device_id=along(dz, head), device_id_type=MESH,
         ).start()
-    count = nz * nc - 1
-    pltpu.make_async_copy(rows_one.at[pl.ds(0, count)], rows_one.at[pl.ds(0, count)], one_recv).wait()
-    genes = rows_one[0]
-    for i in range(1, count + 1):
-        genes = genes + rows_one[i]
-
-    place = x * ny + y
-    samples = depth * nz * FIELDS
-    variance = total(jnp.where(row_lane == at_variance, genes, 0.0)) / samples
-    totals = [
-        pltpu.roll(genes, lax.rem(place * genes_here - i * genes_here + BLK, BLK), 1)
-        for i in range(len(stats))
-    ]
-    here = jnp.logical_and(row_lane >= place * genes_here, row_lane < (place + 1) * genes_here)
-    totals = [jnp.where(here, t, 1.0) for t in totals]
-    burden = totals[0] / jnp.sqrt(variance * totals[1])
-    skat = (totals[2] - variance * totals[3]) / (variance * jnp.sqrt(2.0 * totals[4]))
-    pair_row = lax.broadcasted_iota(jnp.int32, (2, BLK), 0)
-    rows_two[place] = jnp.where(here, jnp.where(pair_row == 0, burden, skat), 0.0)
-    for peer in across_peers:
-        pltpu.make_async_remote_copy(
-            src_ref=rows_two.at[place], dst_ref=rows_two.at[place], send_sem=two_send, recv_sem=two_recv,
-            device_id=across(*peer), device_id_type=MESH,
-        ).start()
-    count = nx * ny - 1
-    pltpu.make_async_copy(rows_two.at[pl.ds(0, count)], rows_two.at[pl.ds(0, count)], two_recv).wait()
-    scores = rows_two[0]
-    for i in range(1, count + 1):
-        scores = scores + rows_two[i]
-    out[...] = scores
+
+    for dz in range(1, nz):
+        send_row(dz)
+
+    @pl.when(c != head)
+    def _():
+        send_row(0)
+
+    def added(rows_ref, base):
+        genes = rows_ref[base]
+        for i in range(1, group):
+            genes = genes + rows_ref[base + i]
+        return genes
+
+    def scored(genes):
+        lane_id = lax.broadcasted_iota(jnp.int32, genes.shape, 1)
+        variance = jnp.sum(jnp.where(lane_id == at_variance, genes, 0.0), axis=1, keepdims=True) / samples
+        totals = [genes] + [pltpu.roll(genes, BLK - i * genes_here, 1) for i in range(1, len(stats))]
+        here = lane_id < genes_here
+        totals = [jnp.where(here, t, 1.0) for t in totals]
+        burden = totals[0] / jnp.sqrt(variance * totals[1])
+        skat = (totals[2] - variance * totals[3]) / (variance * jnp.sqrt(2.0 * totals[4]))
+        return [jnp.where(here, a, 0.0) for a in (burden, skat)]
+
+    def finish(first_rows):
+        lane_id = lax.broadcasted_iota(jnp.int32, (places, BLK), 1)
+        place_id = lax.broadcasted_iota(jnp.int32, (places, BLK), 0)
+        genes = jnp.concatenate([first_rows] + [added(rows_all, p * group) for p in range(1, places)], axis=0)
+        for i, spread in enumerate(scored(genes)):
+            width = genes_here
+            while width < BLK:
+                spread = spread + pltpu.roll(spread, width, 1)
+                width *= 2
+            spread = jnp.where(lane_id // genes_here == place_id, spread, 0.0)
+            out[i : i + 1] = jnp.sum(spread, axis=0, keepdims=True)
+
+    def merge():
+        scores = rows_two[0]
+        for i in range(1, places):
+            scores = scores + rows_two[i]
+        out[...] = scores
+
+    def two_wait(count, sem):
+        span = rows_two.at[pl.ds(0, count)]
+        pltpu.make_async_copy(span, span, sem).wait()
+
+    with_first = jnp.logical_and(z == 0, c == head)
+    across_peers = [(dx, dy) for dx in range(nx) for dy in range(ny)]
+
+    @pl.when(c == head)
+    def _():
+        span = rows_one.at[pl.ds(0, group - 1)]
+        pltpu.make_async_copy(span, span, one_recv).wait()
+        own_genes = added(rows_one, 0)
+        pair_row = lax.broadcasted_iota(jnp.int32, (2, BLK), 0)
+        burden, skat = (pltpu.roll(a, place * genes_here, 1) for a in scored(own_genes))
+        rows_two[place] = jnp.where(pair_row == 0, burden, skat)
+
+        def send_scores(to):
+            pltpu.make_async_remote_copy(
+                src_ref=rows_two.at[place], dst_ref=rows_two.at[place], send_sem=two_send, recv_sem=two_recv,
+                device_id=to, device_id_type=MESH,
+            ).start()
+
+        for core in range(nc):
+            for dx, dy in across_peers[::-1]:
+                to = across(dx, dy, core)
+                if core != head:
+                    send_scores(to)
+                elif dx + dy > 0:
+                    pl.when(jnp.logical_not(with_first & (to[0] + to[3] == 0)))(
+                        functools.partial(send_scores, to)
+                    )
+
+        @pl.when(is_first)
+        def _():
+            span = rows_all.at[pl.ds(0, group * (places - 1))]
+            pltpu.make_async_copy(span, span, row_recv).wait()
+            finish(own_genes)
+
+        @pl.when(jnp.logical_not(is_first))
+        def _():
+            two_wait(places - 1, two_recv)
+            merge()
+
+        skipped = with_first & jnp.logical_not(is_first)
+
+        two_wait(places, two_send)
+        pl.when(skipped)(lambda: two_wait(places - 2, two_send))
+        pl.when(jnp.logical_not(skipped))(lambda: two_wait(places - 1, two_send))
+
+    @pl.when(c != head)
+    def _():
+        two_wait(places, two_recv)
+        merge()
+        pltpu.make_async_copy(rows_one.at[0], rows_one.at[0], one_send).wait()
 
     sent = len(near_peers)
     span = side_in.at[pl.ds(0, sent)]
@@ -264,10 +369,12 @@
     span = words.at[:, pl.ds(0, sent)]
     pltpu.make_async_copy(span, span, word_send).wait()
     pltpu.make_async_copy(gathered, gathered, part_send).wait()
-    span = rows_one.at[pl.ds(0, len(along_peers))]
+    span = rows_one.at[pl.ds(0, nz - 1)]
     pltpu.make_async_copy(span, span, one_send).wait()
-    span = rows_two.at[pl.ds(0, len(across_peers))]
-    pltpu.make_async_copy(span, span, two_send).wait()
+
+    @pl.when(place != 0)
+    def _():
+        pltpu.make_async_copy(rows_all.at[0], rows_all.at[0], row_send).wait()
 
 
 def local(
@@ -311,8 +418,9 @@
             pltpu.VMEM(args[6].shape, jnp.int32),
             pltpu.VMEM((nz * nc, 1, BLK), F32),
             pltpu.VMEM((nx * ny, 2, BLK), F32),
+            pltpu.VMEM((nx * ny * nz * nc, 1, BLK), F32),
             dma, dma((2,)), dma((4,)), dma((nz,)), dma, dma, dma,
-            dma, dma, dma, dma, dma, dma,
+            dma, dma, dma, dma, dma, dma, dma, dma,
         ],
         compiler_params=pltpu.CompilerParams(collective_id=0, has_side_effects=True),
     )(*args)

time: 38.2 us -> 37.1 us (0.971)
  Pallas kernels: 37 us -> 35.9 us
    pallas_call x1, Pallas kernels: 37 us -> 35.9 us  [local(): pl.pallas_call(functools.partial(kernel, sizes), out_shape=pltpu.VMEM((2,...]
where the time goes in v4:
time: 37.1 us; the launch traced here: 37 us
  Pallas kernels  35.9 us (97%)
  between operations  0.64 us (2%)
  local copies, waits for them, and re-layouts  0.52 us (1%)
    pallas_call x1, Pallas kernels, local(): pl.pallas_call(functools.partial(kernel, sizes), out_shape=pltpu.VMEM((2,...  35.9 us

profile of v4, /device:TPU:1, one launch (start us, length us, event | category | flops | bytes accessed | tf_op | source)
XLA Modules:
  0.0 37.0 jit_solution(6370249322423582674)
XLA Ops:
  0.6 35.9 %shard_map.86 = f32[2,128]{1,0:T(2,128)S(1)} custom-call(s32[32,8192]{1,0:T(8,128)} %genotypes.1, f32[64,128]{1,0:T(8,128)} %bitcast.8, f32[16,32]{1,0:T(8,128)} %weight.1, f32[16,32]{1,0:T(8,128)} %residual.1, f32[64,128]{1,0:T(8,128)} %bitcast.9, s32[2,128]{1,0:T(2,128)} %bitcast.10, s32[1,128]{1,0:T(1,128)} %bitcast.11), custom_call_target="tpu_custom_call" | custom-call | tf_op jit(solution)/shard_map/pallas_call | solution.py:399
  36.5 0.5 %slice_bitcast_fusion = (f32[128]{0:T(128)}, f32[128]{0:T(128)}) fusion(f32[2,128]{1,0:T(2,128)S(1)} %shard_map.86), kind=kLoop, calls=%fused_computation | loop fusion | bytes 2048 | tf_op jit(solution)/shard_map/squeeze | solution.py:427

commit v5 on v4

--- a/solution.py
+++ b/solution.py
@@ -16,6 +16,7 @@
 F32 = jnp.float32
 BF16 = jnp.bfloat16
 TAIL = 8
+LINE_AT = 2
 
 
 def total(x):
@@ -31,7 +32,9 @@
 def kernel(
     sizes, genotypes, freq, weight, residual, variant_weight, block_gene, gene_variants, out,
     staged, words, side_staged, side_in, rhs, lhs, scale, tail, part, gathered, freq_v, vw_v, bg_v, gv_v,
-    rows_one, rows_two, rows_all, stage_sem, side_sem, small_sem, word_recv, word_send, side_recv, side_send,
+    rows_one, rows_two, rows_all,
+    line_side, line_words, line_rhs, line_lhs, line_scale, line_tail, line_part, line_in, result,
+    line_side_recv, line_side_send, line_recv, line_send, line_part_recv, line_part_send, stage_sem, side_sem, small_sem, word_recv, word_send, side_recv, side_send,
     part_recv, part_send, one_recv, one_send, two_recv, two_send, row_recv, row_send,
 ):
     ny, nz, nc, nx = sizes
@@ -78,27 +81,30 @@
             pl.semaphore_signal(barrier, inc=1, device_id=peer, device_id_type=MESH)
 
     greet([near(*p) for p in near_peers])
-    greet([along(dz, c) for dz in range(1, nz)])
+    greet([along(dz, core) for dz in range(1, nz) for core in range(nc)])
     greet([across(*p, head) for p in far_x])
 
-    @pl.when(c == head)
-    def _():
-        greet([along(dz, core) for dz in range(1, nz) for core in range(nc) if core != head])
-
     is_first = jnp.logical_and(x + y + z == 0, c == head)
 
-    def known(y, z, c, x):
+    far_steps = 1
+    far_places = [
+        px * ny + py for px in range(nx) for py in range(ny)
+        if min(px, nx - px) + min(py, ny - py) >= far_steps
+    ]
+    is_far = functools.reduce(jnp.logical_or, [x * ny + y == p for p in far_places])
+
+    def met(y, z, c, x):
         return (x == 0) & ((z == 0) | (y == 0)) | (z == 0) & (c == head)
 
     @pl.when(is_first)
     def _():
         for to in itertools.product(range(ny), range(nz), range(nc), range(nx)):
-            if not known(*to):
+            if to[3] * ny + to[0] in far_places and not met(*to):
                 greet([to])
 
-    at_head = len(near_peers) + nz - 1 + len(far_x) * nc
-    elsewhere = len(near_peers) + (nz - 1) * 2
-    pl.semaphore_wait(barrier, jnp.where(c == head, at_head, elsewhere) + jnp.where(known(y, z, c, x), 0, 1))
+    elsewhere = len(near_peers) + (nz - 1) * nc
+    at_head = elsewhere + len(far_x) * nc
+    pl.semaphore_wait(barrier, jnp.where(c == head, at_head, elsewhere) + jnp.where(is_far & jnp.logical_not(met(y, z, c, x)), 1, 0))
 
     for copy in side_copies:
         copy.wait()
@@ -110,6 +116,50 @@
     for i, src in enumerate((weight, residual)):
         pltpu.make_async_copy(src, side_in.at[mine, i], side_recv).start()
 
+    line = z * nc + c
+    line_core = lax.rem(z, nc)
+    takes_line = c == line_core
+    owns_line = z == y * nc + c
+
+    def line_target(dz):
+        zo = lax.rem(z + dz, nz)
+        return (y, zo, lax.rem(zo, nc), x)
+
+    def line_column(dz):
+        zo = lax.rem(z + dz, nz)
+        return pl.multiple_of(((zo // nc * nz + zo) * nc + lax.rem(zo, nc)) * BLK, BLK)
+
+    def send_side(dz):
+        pltpu.make_async_remote_copy(
+            src_ref=side_staged, dst_ref=line_side.at[line], send_sem=line_side_send, recv_sem=line_side_recv,
+            device_id=line_target(dz), device_id_type=MESH,
+        ).start()
+
+    def send_line(dz):
+        pltpu.make_async_remote_copy(
+            src_ref=staged.at[:, pl.ds(line_column(dz), BLK)], dst_ref=line_words.at[line],
+            send_sem=line_send, recv_sem=line_recv, device_id=line_target(dz), device_id_type=MESH,
+        ).start()
+
+    spread = sorted(range(1, nz), key=lambda d: -min(d, nz - d))
+    for dz in spread:
+        send_side(dz)
+
+    @pl.when(takes_line)
+    def _():
+        for i, src in enumerate((weight, residual)):
+            pltpu.make_async_copy(src, line_side.at[line, i], line_side_recv).start()
+        pltpu.make_async_copy(genotypes.at[:, pl.ds(line_column(0), BLK)], line_words.at[line], line_recv).start()
+
+    @pl.when(jnp.logical_not(takes_line))
+    def _():
+        send_side(0)
+
+    stage.wait()
+    for dz in spread:
+        send_line(dz)
+    pl.when(jnp.logical_not(takes_line))(lambda: send_line(0))
+
     def outward(core):
         middle = nz // 2
         return jnp.where(z < middle, 1, jnp.where(z > middle, -1, 1 - 2 * core))
@@ -119,80 +169,121 @@
         sign = (2 * (j % 2) - 1) * outward(core)
         return lax.rem(z + sign * distance + nz, nz)
 
-    stage.wait()
-
     def send_words(j, carry):
-        for dy, dc in near_peers:
-            to = near(dy, dc)
+        def send(to):
             column = pl.multiple_of(((to[0] * nz + owner_of(j, to[2])) * nc + to[2]) * BLK, BLK)
             pltpu.make_async_remote_copy(
                 src_ref=staged.at[:, pl.ds(column, BLK)], dst_ref=words.at[j, mine],
                 send_sem=word_send, recv_sem=word_recv.at[j],
                 device_id=to, device_id_type=MESH,
             ).start()
-        column = pl.multiple_of(((y * nz + owner_of(j, c)) * nc + c) * BLK, BLK)
-        pltpu.make_async_copy(
-            genotypes.at[:, pl.ds(column, BLK)], words.at[j, mine], word_recv.at[j]
-        ).start()
+
+        for peer in near_peers:
+            to = near(*peer)
+            pl.when(owner_of(j, to[2]) != to[0] * nc + to[2])(functools.partial(send, to))
+
+        @pl.when(owner_of(j, c) != mine)
+        def _():
+            column = pl.multiple_of(((y * nz + owner_of(j, c)) * nc + c) * BLK, BLK)
+            pltpu.make_async_copy(
+                genotypes.at[:, pl.ds(column, BLK)], words.at[j, mine], word_recv.at[j]
+            ).start()
+
         return carry
 
     lax.fori_loop(0, nz, send_words, 0)
 
-    pltpu.make_async_copy(side_in, side_in, side_recv).wait()
-    weight_all, residual_all = (
-        jnp.concatenate([side_in[g, i] for g in range(ny * nc)], axis=1) for i in range(2)
-    )
-    rounded = weight_all.astype(BF16).astype(F32)
-    cross = weight_all * residual_all
-    high = cross.astype(BF16).astype(F32)
-    low = (cross - high).astype(BF16).astype(F32)
-    field = lax.broadcasted_iota(jnp.int32, (FIELDS, 1), 0)
-    inverse = jnp.ones((FIELDS, 1), F32)
-    for k in range(1, FIELDS):
-        inverse = jnp.where(field == k, 0.25 ** min(k, FIELDS - 2), inverse)
-    scale[...] = rounded * (inverse * inverse)
-    extra = [a * inverse for a in (rounded, high, low)]
-    row_id = lax.broadcasted_iota(jnp.int32, (2 * TAIL, depth), 0)
-    for k in range(FIELDS):
-        rows_k = jnp.zeros((2 * TAIL, depth), F32)
-        for i, a in enumerate(extra):
-            rows_k = jnp.where(row_id == i, a[k : k + 1], rows_k)
-        lhs[BLK : BLK + 2 * TAIL, k * depth : (k + 1) * depth] = rows_k.astype(BF16)
-    sums = (total(rounded), total(high + low), total(cross * residual_all))
     lane = lax.broadcasted_iota(jnp.int32, (TAIL, BLK), 1)
     sublane = lax.broadcasted_iota(jnp.int32, (TAIL, BLK), 0)
-    tail_rows = jnp.zeros((TAIL, BLK), F32)
-    for i, s in enumerate(sums):
-        tail_rows = jnp.where(sublane == 3 + i, s, tail_rows)
-    tail[...] = tail_rows
+
+    def prepare(side_ref, lhs_ref, scale_ref, tail_ref):
+        count = side_ref.shape[0]
+        width = count * rows
+        weight_all, residual_all = (
+            jnp.concatenate([side_ref[g, i] for g in range(count)], axis=1) for i in range(2)
+        )
+        rounded = weight_all.astype(BF16).astype(F32)
+        cross = weight_all * residual_all
+        high = cross.astype(BF16).astype(F32)
+        low = (cross - high).astype(BF16).astype(F32)
+        field = lax.broadcasted_iota(jnp.int32, (FIELDS, 1), 0)
+        inverse = jnp.ones((FIELDS, 1), F32)
+        for k in range(1, FIELDS):
+            inverse = jnp.where(field == k, 0.25 ** min(k, FIELDS - 2), inverse)
+        scale_ref[...] = rounded * (inverse * inverse)
+        extra = [a * inverse for a in (rounded, high, low)]
+        row_id = lax.broadcasted_iota(jnp.int32, (2 * TAIL, width), 0)
+        for k in range(FIELDS):
+            rows_k = jnp.zeros((2 * TAIL, width), F32)
+            for i, a in enumerate(extra):
+                rows_k = jnp.where(row_id == i, a[k : k + 1], rows_k)
+            lhs_ref[BLK : BLK + 2 * TAIL, k * width : (k + 1) * width] = rows_k.astype(BF16)
+        tail_rows = jnp.zeros((TAIL, BLK), F32)
+        for i, s in enumerate((total(rounded), total(high + low), total(cross * residual_all))):
+            tail_rows = jnp.where(sublane == 3 + i, s, tail_rows)
+        tail_ref[...] = tail_rows
+
+    pltpu.make_async_copy(side_in, side_in, side_recv).wait()
+    prepare(side_in, lhs, scale, tail)
+
+    @pl.when(takes_line)
+    def _():
+        pltpu.make_async_copy(line_side, line_side, line_side_recv).wait()
+        prepare(line_side, line_lhs, line_scale, line_tail)
+
     fold_down = lax.broadcasted_iota(jnp.int32, (HALF, BLK), 0)
     fold_side = lax.broadcasted_iota(jnp.int32, (HALF, BLK), 1)
     folded = jnp.logical_and(fold_side >= HALF, fold_down >= fold_side - HALF)
 
+    def reduce_block(block, lhs_ref, rhs_ref, scale_ref, tail_ref, to_ref):
+        width = block.shape[0]
+        turned = jnp.transpose(block)
+        for k in range(FIELDS):
+            at = slice(k * width, (k + 1) * width)
+            rhs_ref[at, :] = masked(block, k).astype(BF16)
+            lhs_ref[:BLK, at] = (masked(turned, k) * scale_ref[k : k + 1, :]).astype(BF16)
+        gram = jnp.dot(lhs_ref[...], rhs_ref[...], preferred_element_type=F32)
+        low_rows = gram[HALF:BLK]
+        to_ref[:HALF] = jnp.where(folded, pltpu.roll(gram[:HALF], HALF, 1), low_rows)
+        corner = jnp.sum(jnp.where(fold_side - HALF == fold_down, low_rows, 0.0), axis=0, keepdims=True)
+        to_ref[HALF:] = gram[BLK : BLK + TAIL] + jnp.where(sublane == 6, corner, tail_ref[...])
+
     def partial(j):
         pltpu.make_async_copy(words.at[j], words.at[j], word_recv.at[j]).wait()
-        block = words[j].reshape(depth, BLK)
-        turned = jnp.transpose(block)
-        for k in range(FIELDS):
-            rhs[k * depth : (k + 1) * depth, :] = masked(block, k).astype(BF16)
-            lhs[:BLK, k * depth : (k + 1) * depth] = (masked(turned, k) * scale[k : k + 1, :]).astype(BF16)
-        gram = jnp.dot(lhs[...], rhs[...], preferred_element_type=F32)
-        low_rows = gram[HALF:BLK]
-        part[j, :HALF] = jnp.where(folded, pltpu.roll(gram[:HALF], HALF, 1), low_rows)
-        corner = jnp.sum(jnp.where(fold_side - HALF == fold_down, low_rows, 0.0), axis=0, keepdims=True)
-        part[j, HALF:] = gram[BLK : BLK + TAIL] + jnp.where(sublane == 6, corner, tail[...])
+        reduce_block(words[j].reshape(depth, BLK), lhs, rhs, scale, tail, part.at[j])
 
     def far_block(j, carry):
-        partial(j)
         owner = owner_of(j, c)
-        pltpu.make_async_remote_copy(
-            src_ref=part.at[j], dst_ref=gathered.at[lax.rem(owner - z + nz, nz) - 1], send_sem=part_send, recv_sem=part_recv,
-            device_id=(y, owner, c, x), device_id_type=MESH,
-        ).start()
+
+        @pl.when(owner != mine)
+        def _():
+            partial(j)
+            pltpu.make_async_remote_copy(
+                src_ref=part.at[j], dst_ref=gathered.at[lax.rem(owner - z + nz, nz) - 1],
+                send_sem=part_send, recv_sem=part_recv,
+                device_id=(y, owner, c, x), device_id_type=MESH,
+            ).start()
+
         return carry
 
-    lax.fori_loop(0, nz - 1, far_block, 0)
-    partial(nz - 1)
+    line_at = min(LINE_AT, nz - 1)
+    lax.fori_loop(0, line_at, far_block, 0)
+
+    @pl.when(takes_line)
+    def _():
+        pltpu.make_async_copy(line_words, line_words, line_recv).wait()
+        block = line_words[...].reshape(nz * nc * rows, BLK)
+        reduce_block(block, line_lhs, line_rhs, line_scale, line_tail, line_part)
+
+        @pl.when(jnp.logical_not(owns_line))
+        def _():
+            pltpu.make_async_remote_copy(
+                src_ref=line_part, dst_ref=line_in.at[y], send_sem=line_part_send, recv_sem=line_part_recv,
+                device_id=(z // nc, z, c, x), device_id_type=MESH,
+            ).start()
+
+    lax.fori_loop(line_at, nz - 1, far_block, 0)
+    pl.when(jnp.logical_not(owns_line))(lambda: partial(nz - 1))
 
     for copy in smalls:
         copy.wait()
@@ -208,10 +299,24 @@
     live = (own_block - first) * BLK + row_lane < counted
     effective = jnp.where(live, vw_v[pl.ds(own, 1), :], 0.0)
 
-    pltpu.make_async_copy(gathered, gathered, part_recv).wait()
-    summed = part[nz - 1]
-    for j in range(nz - 1):
-        summed = summed + gathered[j]
+    @pl.when(owns_line)
+    def _():
+        span = line_in.at[pl.ds(0, ny - 1)]
+        pltpu.make_async_copy(span, span, line_part_recv).wait()
+        got = line_part[...]
+        for dy in range(1, ny):
+            got = got + line_in[lax.rem(y + dy, ny)]
+        result[...] = got
+
+    @pl.when(jnp.logical_not(owns_line))
+    def _():
+        pltpu.make_async_copy(gathered, gathered, part_recv).wait()
+        got = part[nz - 1]
+        for j in range(nz - 1):
+            got = got + gathered[j]
+        result[...] = got
+
+    summed = result[...]
     ends = summed[HALF:]
     linear, weight_sum = ends[0:1], ends[3:4]
     score = ends[1:2] + ends[2:3] - doubled * ends[4:5]
@@ -253,11 +358,12 @@
     places = nx * ny
     samples = depth * nz * FIELDS
     rows_one[seat] = row
-
-    @pl.when(place != 0)
+    far_id = sum(i * (place == p).astype(jnp.int32) for i, p in enumerate(far_places))
+
+    @pl.when(is_far)
     def _():
         pltpu.make_async_remote_copy(
-            src_ref=rows_one.at[seat], dst_ref=rows_all.at[place * group + seat], send_sem=row_send, recv_sem=row_recv,
+            src_ref=rows_one.at[seat], dst_ref=rows_all.at[far_id * group + seat], send_sem=row_send, recv_sem=row_recv,
             device_id=(0, 0, head, 0), device_id_type=MESH,
         ).start()
 
@@ -290,23 +396,25 @@
         skat = (totals[2] - variance * totals[3]) / (variance * jnp.sqrt(2.0 * totals[4]))
         return [jnp.where(here, a, 0.0) for a in (burden, skat)]
 
-    def finish(first_rows):
-        lane_id = lax.broadcasted_iota(jnp.int32, (places, BLK), 1)
-        place_id = lax.broadcasted_iota(jnp.int32, (places, BLK), 0)
-        genes = jnp.concatenate([first_rows] + [added(rows_all, p * group) for p in range(1, places)], axis=0)
+    def merge(chosen):
+        scores = rows_two[chosen[0]]
+        for p in chosen[1:]:
+            scores = scores + rows_two[p]
+        return scores
+
+    def finish():
+        genes = jnp.concatenate([added(rows_all, i * group) for i in range(len(far_places))], axis=0)
+        lane_id = lax.broadcasted_iota(jnp.int32, genes.shape, 1)
+        row_id = lax.broadcasted_iota(jnp.int32, genes.shape, 0)
+        place_id = sum(jnp.where(row_id == i, p, 0) for i, p in enumerate(far_places))
+        near_scores = merge([p for p in range(places) if p not in far_places])
         for i, spread in enumerate(scored(genes)):
             width = genes_here
             while width < BLK:
                 spread = spread + pltpu.roll(spread, width, 1)
                 width *= 2
             spread = jnp.where(lane_id // genes_here == place_id, spread, 0.0)
-            out[i : i + 1] = jnp.sum(spread, axis=0, keepdims=True)
-
-    def merge():
-        scores = rows_two[0]
-        for i in range(1, places):
-            scores = scores + rows_two[i]
-        out[...] = scores
+            out[i : i + 1] = near_scores[i : i + 1] + jnp.sum(spread, axis=0, keepdims=True)
 
     def two_wait(count, sem):
         span = rows_two.at[pl.ds(0, count)]
@@ -336,22 +444,24 @@
                 if core != head:
                     send_scores(to)
                 elif dx + dy > 0:
-                    pl.when(jnp.logical_not(with_first & (to[0] + to[3] == 0)))(
+                    pl.when(jnp.logical_not(with_first & is_far & (to[0] + to[3] == 0)))(
                         functools.partial(send_scores, to)
                     )
 
         @pl.when(is_first)
         def _():
-            span = rows_all.at[pl.ds(0, group * (places - 1))]
+            if places - 1 > len(far_places):
+                two_wait(places - 1 - len(far_places), two_recv)
+            span = rows_all.at[pl.ds(0, group * len(far_places))]
             pltpu.make_async_copy(span, span, row_recv).wait()
-            finish(own_genes)
+            finish()
 
         @pl.when(jnp.logical_not(is_first))
         def _():
             two_wait(places - 1, two_recv)
-            merge()
-
-        skipped = with_first & jnp.logical_not(is_first)
+            out[...] = merge(range(places))
+
+        skipped = with_first & is_far
 
         two_wait(places, two_send)
         pl.when(skipped)(lambda: two_wait(places - 2, two_send))
@@ -360,19 +470,37 @@
     @pl.when(c != head)
     def _():
         two_wait(places, two_recv)
-        merge()
+        out[...] = merge(range(places))
         pltpu.make_async_copy(rows_one.at[0], rows_one.at[0], one_send).wait()
 
     sent = len(near_peers)
     span = side_in.at[pl.ds(0, sent)]
     pltpu.make_async_copy(span, span, side_send).wait()
-    span = words.at[:, pl.ds(0, sent)]
+    span = words.at[pl.ds(0, nz - 1), pl.ds(0, sent)]
     pltpu.make_async_copy(span, span, word_send).wait()
-    pltpu.make_async_copy(gathered, gathered, part_send).wait()
+
+    def sent_line(count):
+        for ref, sem in ((line_side, line_side_send), (line_words, line_send)):
+            span = ref.at[pl.ds(0, count)]
+            pltpu.make_async_copy(span, span, sem).wait()
+
+    pl.when(takes_line)(lambda: sent_line(nz - 1))
+    pl.when(jnp.logical_not(takes_line))(lambda: sent_line(nz))
+
+    @pl.when(jnp.logical_and(takes_line, jnp.logical_not(owns_line)))
+    def _():
+        pltpu.make_async_copy(line_part, line_part, line_part_send).wait()
+
+    def sent_parts(count):
+        span = gathered.at[pl.ds(0, count)]
+        pltpu.make_async_copy(span, span, part_send).wait()
+
+    pl.when(owns_line)(lambda: sent_parts(nz - 1))
+    pl.when(jnp.logical_not(owns_line))(lambda: sent_parts(nz - 2))
     span = rows_one.at[pl.ds(0, nz - 1)]
     pltpu.make_async_copy(span, span, one_send).wait()
 
-    @pl.when(place != 0)
+    @pl.when(is_far)
     def _():
         pltpu.make_async_copy(rows_all.at[0], rows_all.at[0], row_send).wait()
 
@@ -419,6 +547,16 @@
             pltpu.VMEM((nz * nc, 1, BLK), F32),
             pltpu.VMEM((nx * ny, 2, BLK), F32),
             pltpu.VMEM((nx * ny * nz * nc, 1, BLK), F32),
+            pltpu.VMEM((nz * nc, 2, FIELDS, rows), F32),
+            pltpu.VMEM((nz * nc, rows, BLK), jnp.int32),
+            pltpu.VMEM((FIELDS * nz * nc * rows, BLK), BF16),
+            pltpu.VMEM((BLK + 2 * TAIL, FIELDS * nz * nc * rows), BF16),
+            pltpu.VMEM((FIELDS, nz * nc * rows), F32),
+            pltpu.VMEM((TAIL, BLK), F32),
+            pltpu.VMEM((HALF + TAIL, BLK), F32),
+            pltpu.VMEM((ny, HALF + TAIL, BLK), F32),
+            pltpu.VMEM((HALF + TAIL, BLK), F32),
+            dma, dma, dma, dma, dma, dma,
             dma, dma((2,)), dma((4,)), dma((nz,)), dma, dma, dma,
             dma, dma, dma, dma, dma, dma, dma, dma,
         ],

time: 37.1 us -> 37.1 us (level)
  no operation moved by 1% of the time
where the time goes in v5:
time: 37.1 us; the launch traced here: 37 us
  Pallas kernels  35.8 us (96%)
  between operations  0.64 us (2%)
  local copies, waits for them, and re-layouts  0.52 us (1%)
    pallas_call x1, Pallas kernels, local(): pl.pallas_call(functools.partial(kernel, sizes), out_shape=pltpu.VMEM((2,...  35.8 us

profile of v5, /device:TPU:1, one launch (start us, length us, event | category | flops | bytes accessed | tf_op | source)
XLA Modules:
  0.0 37.0 jit_solution(4245489250429557666)
XLA Ops:
  0.6 35.8 %shard_map.86 = f32[2,128]{1,0:T(2,128)S(1)} custom-call(s32[32,8192]{1,0:T(8,128)} %genotypes.1, f32[64,128]{1,0:T(8,128)} %bitcast.8, f32[16,32]{1,0:T(8,128)} %weight.1, f32[16,32]{1,0:T(8,128)} %residual.1, f32[64,128]{1,0:T(8,128)} %bitcast.9, s32[2,128]{1,0:T(2,128)} %bitcast.10, s32[1,128]{1,0:T(1,128)} %bitcast.11), custom_call_target="tpu_custom_call" | custom-call | tf_op jit(solution)/shard_map/pallas_call | solution.py:527
  36.5 0.5 %slice_bitcast_fusion = (f32[128]{0:T(128)}, f32[128]{0:T(128)}) fusion(f32[2,128]{1,0:T(2,128)S(1)} %shard_map.86), kind=kLoop, calls=%fused_computation | loop fusion | bytes 2048 | tf_op jit(solution)/shard_map/squeeze | solution.py:565

commit v6 on v5

--- a/solution.py
+++ b/solution.py
@@ -71,7 +71,7 @@
         return (lax.rem(y + dy, ny), z, core, lax.rem(x + dx, nx))
 
     head = nc - 1
-    order = sorted(range(1, ny), key=lambda d: -min(d, ny - d))
+    order = sorted(range(1, ny), key=lambda d: min(d, ny - d))
     near_peers = [(dy, dc) for dy in order + [0] for dc in range(nc) if (dy, dc) != (0, 0)]
     far_x = [(dx, dy) for dx in range(1, nx) for dy in range(ny)]
     barrier = pltpu.get_barrier_semaphore()

time: 37.1 us -> 37 us (level)
  no operation moved by 1% of the time
where the time goes in v6:
time: 37 us
  Pallas kernels  35.8 us (97%)
  between operations  0.64 us (2%)
  local copies, waits for them, and re-layouts  0.52 us (1%)
    pallas_call x1, Pallas kernels, local(): pl.pallas_call(functools.partial(kernel, sizes), out_shape=pltpu.VMEM((2,...  35.8 us

profile of v6, /device:TPU:1, one launch (start us, length us, event | category | flops | bytes accessed | tf_op | source)
XLA Modules:
  0.0 37.0 jit_solution(6618275949671600676)
XLA Ops:
  0.6 35.8 %shard_map.86 = f32[2,128]{1,0:T(2,128)S(1)} custom-call(s32[32,8192]{1,0:T(8,128)} %genotypes.1, f32[64,128]{1,0:T(8,128)} %bitcast.8, f32[16,32]{1,0:T(8,128)} %weight.1, f32[16,32]{1,0:T(8,128)} %residual.1, f32[64,128]{1,0:T(8,128)} %bitcast.9, s32[2,128]{1,0:T(2,128)} %bitcast.10, s32[1,128]{1,0:T(1,128)} %bitcast.11), custom_call_target="tpu_custom_call" | custom-call | tf_op jit(solution)/shard_map/pallas_call | solution.py:527
  36.4 0.5 %slice_bitcast_fusion = (f32[128]{0:T(128)}, f32[128]{0:T(128)}) fusion(f32[2,128]{1,0:T(2,128)S(1)} %shard_map.86), kind=kLoop, calls=%fused_computation | loop fusion | bytes 2048 | tf_op jit(solution)/shard_map/squeeze | solution.py:565
